TPU v7x, 256 devices: a whole 4x4x8 slice. The times are simulated.
256 devices in a mesh: dp: 32 (over x, y, core), mp: 8 (over z).
Axes of the slice: x: 4, y: 4, z: 8, core: 2. Of those that a mesh axis runs over, the one named last changes fastest.
Arguments:
- vit_features: bfloat16 [128, 256, 1024], P('dp', 'mp'), may hold values from -6 to 6
- patch_counts: int32 [128], P('dp'), may hold values from 64 to 192
- text_counts: int32 [128], P('dp'), may hold values from 1 to 63
- tile_dest: int32 [128], P('dp'), may hold values from 0 to 31, as said below
- text_embeds: bfloat16 [128, 256, 4096], P('dp', 'mp'), may hold values from -6 to 6
- w_proj: bfloat16 [1024, 4096], replicated, may hold values from -0.1875 to 0.1875
- b_proj: float32 [4096], replicated, may hold values from -3 to 3
- norm_gain: float32 [1, 4096], replicated, may hold values from 0.1 to 1.9
- w_qkv: bfloat16 [1, 4096, 8, 512], P(None, 'dp', 'mp'), may hold values from -0.375 to 0.375
- w_out: bfloat16 [1, 8, 256, 4096], P(None, 'mp', None, 'dp'), may hold values from -0.125 to 0.125
Outputs:
- hidden_out: bfloat16 [128, 256, 4096], P('dp', 'mp')
Inputs may be any that keep to these rules, and one draw needn't show every extreme that they name: `tile_dest`: each language-model rank receives exactly 4 tiles; one source rank sends at most 2 tiles to one language-model rank, and every source rank sends 2 to some rank.
All inputs are finite; a program needn't handle non-finite values.
Results may differ from a plain program's by a relative error of at most 0.01.
Values may be sent and summed in bfloat16 or wider, within the bound.
No kernel may reach another device: no remote copies, remote signals or barrier semaphores. Data moves between devices by JAX's collectives and lax.ppermute only.
A program may use at most 128 MiB of HBM per device.

v0:
```python
import math
import jax
import jax.numpy as jnp
from jax import lax
from jax.sharding import PartitionSpec as P

HS = 128
GROUP = 2
CAP = 2
rope_base = 500000.0
epsilon = 1e-05


def sent_to_all(shard, axis):
    copies = jnp.broadcast_to(shard, (lax.axis_size(axis), *shard.shape))
    return lax.all_to_all(copies, axis, split_axis=0, concat_axis=0, tiled=True)


def joined_along(parts, dim):
    lengths = list(parts.shape[1:])
    lengths[dim] *= parts.shape[0]
    return jnp.moveaxis(parts, 0, dim).reshape(lengths)


def collect(shard, axis, dim):
    parts = sent_to_all(shard, axis)
    return joined_along(parts, dim)


def gather_turned(arrays, axis, dims):
    turned = [jnp.moveaxis(a, dim, 0) for a, dim in zip(arrays, dims)]
    both = jnp.concatenate([t.reshape(len(t), -1) for t in turned], axis=1)
    result, at, gathered = (lax.all_gather(both, axis, axis=0, tiled=True), 0, [])
    for t, dim in zip(turned, dims):
        section = result[:, at : at + t[0].size].reshape(-1, *t.shape[1:])
        gathered.append(jnp.moveaxis(section, 0, dim))
        at += t[0].size
    return tuple(gathered)


def tile_angles(tile_size, head_size):
    half_size = head_size // 2
    inverse = jnp.exp(
        -(2.0 * jnp.arange(half_size, dtype=jnp.float32) / head_size) * math.log(rope_base)
    )
    positions = jnp.arange(tile_size, dtype=jnp.float32)
    return positions[:, None] * inverse[None, :]


def rotate_half(values, angles):
    half_size = values.shape[-1] // 2
    cosine = jnp.cos(angles)
    sine_part = jnp.sin(angles)
    first_half = values[..., :half_size]
    second = values[..., half_size:]
    return jnp.concatenate(
        [first_half * cosine - second * sine_part, second * cosine + first_half * sine_part],
        axis=-1,
    )


def slot_table(full_dest, dest_ids):
    full_hot = (full_dest[:, None] == dest_ids[None, :]).astype(jnp.int32)
    return jnp.sum((jnp.cumsum(full_hot, axis=0) - full_hot) * full_hot, axis=1)


def send_capped(vit_features, tile_dest, own_before, full_dest, full_slots, rank_count, my_rank):
    image_count, local_rows, vision_width = vit_features.shape
    targets = tile_dest * CAP + own_before
    placing = (targets[:, None] == jnp.arange(rank_count * CAP, dtype=jnp.int32)[None, :]).astype(
        jnp.bfloat16
    )
    flat_rows = vit_features.reshape(image_count, local_rows * vision_width)
    outgoing = jnp.dot(placing.T, flat_rows, preferred_element_type=jnp.float32).astype(
        jnp.bfloat16
    )
    outgoing = outgoing.reshape(rank_count, CAP, local_rows, vision_width)
    incoming = lax.all_to_all(outgoing, "dp", split_axis=0, concat_axis=0, tiled=True)
    image_total = full_dest.shape[0]
    dest_ids = jnp.arange(rank_count, dtype=jnp.int32)
    by_source = full_dest.reshape(rank_count, image_count)
    source_hot = (by_source[:, :, None] == dest_ids[None, None, :]).astype(jnp.int32)
    source_before = jnp.sum(
        (jnp.cumsum(source_hot, axis=1) - source_hot) * source_hot, axis=2
    ).reshape(image_total)
    columns = jnp.arange(image_total, dtype=jnp.int32) // image_count * CAP + source_before
    mine_mask = full_dest == my_rank
    pick_rows = (
        mine_mask[None, :]
        & (full_slots[None, :] == jnp.arange(image_count, dtype=jnp.int32)[:, None])
    ).astype(jnp.bfloat16)
    pick_cols = (columns[:, None] == jnp.arange(rank_count * CAP, dtype=jnp.int32)[None, :]).astype(
        jnp.bfloat16
    )
    selector = jnp.dot(pick_rows, pick_cols, preferred_element_type=jnp.float32).astype(
        jnp.bfloat16
    )
    arrived = jnp.dot(
        selector,
        incoming.reshape(rank_count * CAP, local_rows * vision_width),
        preferred_element_type=jnp.float32,
    )
    return arrived.astype(jnp.bfloat16).reshape(image_count, local_rows, vision_width)


def layer_step(hidden, gain_row, weights_qkv, weights_out, lengths, angles):
    as_float = hidden.astype(jnp.float32)
    mean_square = jnp.mean(as_float * as_float, axis=-1, keepdims=True)
    normed = (as_float * lax.rsqrt(mean_square + epsilon) * gain_row).astype(jnp.bfloat16)
    full_rows = lax.all_gather(normed, "mp", axis=1, tiled=True)
    image_count, tile_size, model_width = full_rows.shape
    head_count = weights_qkv.shape[1]
    joined_rows = jnp.dot(
        full_rows.reshape(image_count * tile_size, model_width),
        weights_qkv.reshape(model_width, -1),
        preferred_element_type=jnp.float32,
    )
    joined_rows = joined_rows.reshape(image_count, tile_size, head_count, GROUP + 2, HS)
    queries = rotate_half(joined_rows[:, :, :, :GROUP, :], angles[None, :, None, None, :]).astype(
        jnp.bfloat16
    )
    key_heads = rotate_half(joined_rows[:, :, :, GROUP, :], angles[None, :, None, :]).astype(
        jnp.bfloat16
    )
    value_heads = joined_rows[:, :, :, GROUP + 1, :].astype(jnp.bfloat16)
    score_scale = 1.0 / math.sqrt(HS)
    scores = (
        jnp.einsum("brhge,bche->bhgrc", queries, key_heads, preferred_element_type=jnp.float32)
        * score_scale
    )
    row_ids = jnp.arange(tile_size, dtype=jnp.int32)[:, None]
    col_ids = jnp.arange(tile_size, dtype=jnp.int32)[None, :]
    allowed = (col_ids <= row_ids)[None, None, None, :, :] & (
        col_ids[None, None, None, :, :] < lengths[:, None, None, None, None]
    )
    scores = jnp.where(allowed, scores, -1e30)
    row_max = jnp.max(scores, axis=-1, keepdims=True)
    weights = jnp.where(allowed, jnp.exp(scores - row_max), 0.0)
    probabilities = (weights / jnp.sum(weights, axis=-1, keepdims=True)).astype(jnp.bfloat16)
    attended = jnp.einsum(
        "bhgrc,bche->brhge", probabilities, value_heads, preferred_element_type=jnp.float32
    ).astype(jnp.bfloat16)
    head_term = jnp.dot(
        attended.reshape(image_count * tile_size, -1),
        weights_out.reshape(-1, model_width),
        preferred_element_type=jnp.float32,
    )
    head_term = head_term.reshape(image_count, tile_size, model_width)
    summed = lax.psum_scatter(
        head_term.astype(jnp.bfloat16), "mp", scatter_dimension=1, tiled=True
    ).astype(jnp.float32)
    return (as_float + summed).astype(jnp.bfloat16)


def body(
    vit_features,
    patch_counts,
    text_counts,
    tile_dest,
    text_embeds,
    w_proj,
    b_proj,
    norm_gain,
    w_qkv,
    w_out,
):
    rank_count = lax.axis_size("dp")
    my_rank = lax.axis_index("dp")
    image_count, local_rows, vision_width = vit_features.shape
    dest_ids = jnp.arange(rank_count, dtype=jnp.int32)
    own_hot = (tile_dest[:, None] == dest_ids[None, :]).astype(jnp.int32)
    own_before = jnp.sum((jnp.cumsum(own_hot, axis=0) - own_hot) * own_hot, axis=1)
    full_dest = collect(tile_dest, "dp", 0)
    full_slots = slot_table(full_dest, dest_ids)
    arrived = send_capped(
        vit_features, tile_dest, own_before, full_dest, full_slots, rank_count, my_rank
    )
    mp_rank = lax.axis_index("mp")
    projected = (
        jnp.dot(
            arrived.reshape(image_count * local_rows, vision_width),
            w_proj,
            preferred_element_type=jnp.float32,
        )
        + b_proj
    )
    projected = projected.reshape(image_count, local_rows, -1)
    row_ids = (mp_rank * local_rows + jnp.arange(local_rows, dtype=jnp.int32))[None, :, None]
    image_end = patch_counts[:, None, None]
    text_end = (patch_counts + text_counts)[:, None, None]
    hidden = jnp.where(
        row_ids < image_end,
        projected,
        jnp.where(row_ids < text_end, text_embeds.astype(jnp.float32), 0.0),
    ).astype(jnp.bfloat16)
    lengths = patch_counts + text_counts
    all_qkv, all_out = gather_turned((w_qkv, w_out), "dp", (1, 3))
    tile_size = local_rows * lax.axis_size("mp")
    angles = tile_angles(tile_size, HS)
    hidden = layer_step(hidden, norm_gain[0], all_qkv[0], all_out[0], lengths, angles)
    return hidden


def solution(mesh):
    in_specs = (
        P("dp", "mp", None),
        P("dp"),
        P("dp"),
        P("dp"),
        P("dp", "mp", None),
        P(),
        P(),
        P(),
        P(None, "dp", "mp", None),
        P(None, "mp", None, "dp"),
    )
    out_specs = P("dp", "mp", None)
    return jax.shard_map(body, mesh=mesh, in_specs=in_specs, out_specs=out_specs, check_vma=False)
```

profile of v0, /device:TPU:1, one launch (start us, length us, event | category | flops | bytes accessed | tf_op | source)
XLA Modules:
  0.0 328.6 jit_solution(4973166637287278460)
XLA Ops:
  6.5 1.0 copy.34
  7.6 1.5 pad_maximum_fusion
  9.1 1.3 broadcast_in_dim.37
  10.4 8.6 %all-to-all-start = ((s32[32,1,4]{2,1,0:T(1,128)}), s32[32,1,4]{2,1,0:T(1,128)S(1)}, u32[]{:S(2)}, u32[]{:S(2)}) async-start(s32[32,1,4]{2,1,0:T(1,128)} %broadcast_in_dim.37), calls=%async_computation | async-start | bytes 32768 | tf_op jit(solution)/shard_map/all_to_all | solution.py:16
  19.0 1.2 copy.47
  20.2 0.7 fusion.33
  20.9 0.8 select_reduce_fusion.1
  21.8 0.7 multiply_add_fusion
  22.4 1.4 convolution_convert_fusion
  23.8 4.4 %copy.48 = bf16[8,8,32,1024]{3,2,1,0:T(8,128)(2,1)} copy(bf16[8,8,32,1024]{3,1,2,0:T(8,128)(2,1)S(1)} %bitcast.93) | data formatting | bytes 8388608
  28.2 7.6 %all-to-all-start.1 = ((bf16[32,2,32,1024]{3,2,1,0:T(8,128)(2,1)}), bf16[32,2,32,1024]{3,2,1,0:T(8,128)(2,1)}, u32[]{:S(2)}, u32[]{:S(2)}) async-start(bf16[32,2,32,1024]{3,2,1,0:T(8,128)(2,1)} %bitcast.91), calls=%async_computation.1 | async-start | bytes 8388608 | tf_op jit(solution)/shard_map/all_to_all | solution.py:78
  36.0 0.5 broadcast.235
  36.5 0.7 reduce.5
  37.7 0.3 fusion.48
  38.3 54.8 %all-to-all-done.1 = bf16[32,2,32,1024]{3,2,1,0:T(8,128)(2,1)} async-done(((bf16[32,2,32,1024]{3,2,1,0:T(8,128)(2,1)}), bf16[32,2,32,1024]{3,2,1,0:T(8,128)(2,1)}, u32[]{:S(2)}, u32[]{:S(2)}) %all-to-all-start.1) | async-done | bytes 4194336 | tf_op jit(solution)/shard_map/all_to_all | solution.py:78
  93.2 7.0 %copy.49 = bf16[8,8,32,1024]{3,1,2,0:T(8,128)(2,1)} copy(bf16[8,8,32,1024]{3,2,1,0:T(8,128)(2,1)} %bitcast.51) | data formatting | bytes 8388608
  100.1 3.2 convolution_convert_fusion.1
  103.5 4.7 %convolution_add_fusion = bf16[128,4096]{1,0:T(8,128)(2,1)S(1)} fusion(bf16[128,1024]{1,0:T(8,128)(2,1)S(1)} %reshape_reshape.3, bf16[1024,4096]{1,0:T(8,128)(2,1)} %param.15, f32[4096]{0:T(1024)S(1)} %copy-done.1), kind=kOutput, calls=%fused_computation.5 | convolution fusion | flops 1074790400 | bytes 9715712 | tf_op jit(solution)/shard_map/dot_general | solution.py:180
  108.3 0.6 fusion.2
  109.0 1.3 fusion.4
  110.3 0.2 reduce-scatter.2.cloned.1.call-start
  110.7 0.3 fusion.27
  111.0 0.2 broadcast_and_fusion
  111.2 4.7 %slice.36 = bf16[4096,512]{0,1:T(8,128)(2,1)} slice(bf16[4096,768]{0,1:T(8,128)(2,1)} %all-gather.5.cloned.1.call-done), slice={[0:4096], [0:512]} | slice | bytes 8388608 | tf_op jit(solution)/shard_map/slice | solution.py:35
  115.9 92.3 %all-gather.3.cloned.1.call-done = bf16[4,256,4096]{2,1,0:T(8,128)(2,1)} async-done(((bf16[4,32,4096]{2,1,0:T(8,128)(2,1)}), bf16[4,256,4096]{2,1,0:T(8,128)(2,1)}) %all-gather.3.cloned.1.call-update) | async-done | bytes 8388624 | tf_op jit(solution)/shard_map/all_gather | solution.py:110
  208.2 8.2 %fusion.7 = f32[4,256,1,4,128]{1,4,3,0,2:T(8,128)S(1)} fusion(bf16[4,128,4096,1]{2,1,0,3:T(8,128)(2,1)} %bitcast.94, bf16[4,256,4096]{2,1,0:T(8,128)(2,1)} %all-gather.3.cloned.1.call-done), kind=kOutput, calls=%fused_computation.19 | convolution fusion | flops 4294967296 | bytes 14680064 | tf_op jit(solution)/shard_map/dot_general | solution.py:113
  216.7 0.5 fusion.6
  217.2 0.6 fusion.10
  217.8 0.8 convolution_convert_fusion.3
  218.6 7.2 %convolution_convert_fusion.2 = bf16[4,256,4096]{2,1,0:T(8,128)(2,1)} fusion(bf16[4,256,256]{1,2,0:T(8,128)(2,1)S(1)} %bitcast.96, bf16[4096,768]{0,1:T(8,128)(2,1)} %all-gather.5.cloned.1.call-done), kind=kOutput, calls=%fused_computation.4 | convolution fusion | flops 2151677952 | bytes 11010048 | tf_op jit(solution)/shard_map/dot_general | solution.py:143
  225.8 93.8 %reduce-scatter.2.cloned.1.call-done = bf16[4,32,4096]{2,1,0:T(8,128)(2,1)} async-done(((bf16[4,256,4096]{2,1,0:T(8,128)(2,1)}), bf16[4,32,4096]{2,1,0:T(8,128)(2,1)}) %reduce-scatter.2.cloned.1.call-update) | async-done | bytes 1048592 | tf_op jit(solution)/shard_map/reduce_scatter | solution.py:149
  319.6 2.4 fusion.5
  (38 shorter events, 1.7 us)
Async XLA Ops:
  6.5 104.7 %all-gather.5.cloned.1.call-start = ((), (), s32[]{:S(2)}) async-start(), calls=%async_computation.4 | async-start | bytes 6488064 | tf_op jit(solution)/shard_map/all_gather | solution.py:33
  10.4 17.8 %all-to-all-start = ((s32[32,1,4]{2,1,0:T(1,128)}), s32[32,1,4]{2,1,0:T(1,128)S(1)}, u32[]{:S(2)}, u32[]{:S(2)}) async-start(s32[32,1,4]{2,1,0:T(1,128)} %broadcast_in_dim.37), calls=%async_computation | async-start | bytes 32768 | tf_op jit(solution)/shard_map/all_to_all | solution.py:16
  28.2 7.6 %copy-start.3 = (s32[4]{0:T(128)S(1)}, s32[4]{0:T(128)}, u32[]{:S(2)}) copy-start(s32[4]{0:T(128)} %param.11) | copy-start | bytes 52
  28.2 7.6 %copy-start.4 = (s32[4]{0:T(128)S(1)}, s32[4]{0:T(128)}, u32[]{:S(2)}) copy-start(s32[4]{0:T(128)} %param.12) | copy-start | bytes 52
  28.2 64.9 %all-to-all-start.1 = ((bf16[32,2,32,1024]{3,2,1,0:T(8,128)(2,1)}), bf16[32,2,32,1024]{3,2,1,0:T(8,128)(2,1)}, u32[]{:S(2)}, u32[]{:S(2)}) async-start(bf16[32,2,32,1024]{3,2,1,0:T(8,128)(2,1)} %bitcast.91), calls=%async_computation.1 | async-start | bytes 8388608 | tf_op jit(solution)/shard_map/all_to_all | solution.py:78
  35.8 172.4 %all-gather.3.cloned.1.call-start = ((), (), s32[]{:S(2)}) async-start(), calls=%async_computation.3 | async-start | bytes 9437184 | tf_op jit(solution)/shard_map/all_gather | solution.py:110
  100.1 3.4 %copy-start.1 = (f32[4096]{0:T(1024)S(1)}, f32[4096]{0:T(1024)}, u32[]{:S(2)}) copy-start(f32[4096]{0:T(1024)} %param.16) | copy-start | bytes 49156
  103.5 4.8 %copy-start = (bf16[4,32,4096]{2,1,0:T(8,128)(2,1)S(1)}, bf16[4,32,4096]{2,1,0:T(8,128)(2,1)}, u32[]{:S(2)}) copy-start(bf16[4,32,4096]{2,1,0:T(8,128)(2,1)} %param.14) | copy-start | bytes 3145732
  108.3 0.7 copy-start.2
  110.3 209.3 %reduce-scatter.2.cloned.1.call-start = ((), (), s32[]{:S(2)}) async-start(), calls=%async_computation.5 | async-start | bytes 9437184 | tf_op jit(solution)/shard_map/reduce_scatter | solution.py:149
Sparse Core Ops, SparseCore 0:
  9.8 94.2 all-gather.4
  110.4 97.6 all-gather.2
  225.9 93.6 reduce-scatter.1
where the time goes:
time: 329 us
  waiting for transfers between devices  241 us (73%)
  matrix products  26 us (8%)
  local copies, waits for them, and re-layouts  20.7 us (6%)
  starting transfers between devices  16.4 us (5%)
  between operations  13.3 us (4%)
  other arithmetic  11.1 us (3%)
    reduce_scatter x1, waiting for transfers between devices, layer_step(): lax.psum_scatter(head_term.astype(jnp.bfloat16), 'mp', scatter_dimension=...  93.8 us
    all_gather x1, waiting for transfers between devices, layer_step(): full_rows = lax.all_gather(normed, 'mp', axis=1, tiled=True)  92.3 us
    all_to_all x1, waiting for transfers between devices, send_capped(): lax.all_to_all(outgoing, 'dp', split_axis=0, concat_axis=0, tiled=True)  54.8 us
    unnamed x14, local copies, waits for them, and re-layouts  13.7 us
    all_to_all x1, starting transfers between devices, sent_to_all(): return lax.all_to_all(copies, axis, split_axis=0, concat_axis=0, tiled=True)  8.58 us
    dot_general x1, matrix products, layer_step(): jnp.dot(full_rows.reshape(image_count * tile_size, model_width), weights_...  8.21 us
    all_to_all x1, starting transfers between devices, send_capped(): lax.all_to_all(outgoing, 'dp', split_axis=0, concat_axis=0, tiled=True)  7.57 us
    dot_general x1, matrix products, layer_step(): jnp.dot(attended.reshape(image_count * tile_size, -1), weights_out.reshap...  7.19 us
  transfers between devices with their start and end apart: 5, of which 3 were waited for; matrix products, arithmetic and copies ran while one was open for 11% of the time, Pallas kernels for 0%

commit v1 on v0

--- a/solution.py
+++ b/solution.py
@@ -107,7 +107,9 @@
     as_float = hidden.astype(jnp.float32)
     mean_square = jnp.mean(as_float * as_float, axis=-1, keepdims=True)
     normed = (as_float * lax.rsqrt(mean_square + epsilon) * gain_row).astype(jnp.bfloat16)
-    full_rows = lax.all_gather(normed, "mp", axis=1, tiled=True)
+    full_rows = jnp.concatenate(
+        lax.all_to_all(jnp.stack([normed] * lax.axis_size("mp")), "mp", 0, 0), axis=1
+    )
     image_count, tile_size, model_width = full_rows.shape
     head_count = weights_qkv.shape[1]
     joined_rows = jnp.dot(

time: 329 us -> 426 us (1.29)
  waiting for transfers between devices: 241 us -> 320 us
  local copies, waits for them, and re-layouts: 20.7 us -> 31.6 us
  starting transfers between devices: 16.4 us -> 24.8 us
    all_to_all x0 -> x1, waiting for transfers between devices: none -> 119 us  [layer_step(): lax.all_to_all(jnp.stack([normed] * lax.axis_size('mp')), 'mp', 0, 0)]
    all_gather x1 -> x0, waiting for transfers between devices: 92.3 us -> none  [layer_step(): full_rows = lax.all_gather(normed, 'mp', axis=1, tiled=True)]
    all_gather x1, waiting for transfers between devices: 0.02 us -> 61.8 us  [gather_turned(): lax.all_gather(both, axis, axis=0, tiled=True)]
    all_to_all x0 -> x1, starting transfers between devices: none -> 8.32 us  [layer_step(): lax.all_to_all(jnp.stack([normed] * lax.axis_size('mp')), 'mp', 0, 0)]
    reshape x0 -> x1, local copies, waits for them, and re-layouts: none -> 7.7 us  [layer_step(): jnp.concatenate(lax.all_to_all(jnp.stack([normed] * lax.axis_size('mp')),...]
    all_to_all x1, waiting for transfers between devices: 54.8 us -> 49.7 us  [send_capped(): lax.all_to_all(outgoing, 'dp', split_axis=0, concat_axis=0, tiled=True)]
    unnamed x14 -> x18, local copies, waits for them, and re-layouts: 13.7 us -> 12.6 us
  transfers between devices with their start and end apart: 5 -> 5, of which waited for: 3 -> 4; matrix products, arithmetic and copies ran while one was open for 11% -> 4% of each run, Pallas kernels for 0% -> 0%
where the time goes in v1:
time: 426 us
  waiting for transfers between devices  320 us (75%)
  local copies, waits for them, and re-layouts  31.6 us (7%)
  matrix products  25.9 us (6%)
  starting transfers between devices  24.8 us (6%)
  between operations  13.7 us (3%)
  other arithmetic  9.23 us (2%)
    all_to_all x1, waiting for transfers between devices, layer_step(): lax.all_to_all(jnp.stack([normed] * lax.axis_size('mp')), 'mp', 0, 0)  119 us
    reduce_scatter x1, waiting for transfers between devices, layer_step(): lax.psum_scatter(head_term.astype(jnp.bfloat16), 'mp', scatter_dimension=...  90.2 us
    all_gather x1, waiting for transfers between devices, gather_turned(): lax.all_gather(both, axis, axis=0, tiled=True)  61.8 us
    all_to_all x1, waiting for transfers between devices, send_capped(): lax.all_to_all(outgoing, 'dp', split_axis=0, concat_axis=0, tiled=True)  49.7 us
    unnamed x18, local copies, waits for them, and re-layouts  12.6 us
    all_to_all x1, starting transfers between devices, sent_to_all(): return lax.all_to_all(copies, axis, split_axis=0, concat_axis=0, tiled=True)  8.57 us
  transfers between devices with their start and end apart: 5, of which 4 were waited for; matrix products, arithmetic and copies ran while one was open for 4% of the time, Pallas kernels for 0%

profile of v1, /device:TPU:1, one launch (start us, length us, event | category | flops | bytes accessed | tf_op | source)
XLA Modules:
  0.0 425.6 jit_solution(8515496710684595112)
XLA Ops:
  6.5 1.3 broadcast_in_dim.37
  7.8 8.6 %all-to-all-start = ((s32[32,1,4]{2,1,0:T(1,128)}), s32[32,1,4]{2,1,0:T(1,128)S(1)}, u32[]{:S(2)}, u32[]{:S(2)}) async-start(s32[32,1,4]{2,1,0:T(1,128)} %broadcast_in_dim.37), calls=%async_computation | async-start | bytes 32768 | tf_op jit(solution)/shard_map/all_to_all | solution.py:16
  16.4 0.7 fusion.28
  17.1 1.2 copy.49
  18.3 0.8 select_reduce_fusion.1
  19.1 0.7 multiply_add_fusion
  19.8 1.4 convolution_convert_fusion
  21.2 4.4 %copy.50 = bf16[8,8,32,1024]{3,2,1,0:T(8,128)(2,1)} copy(bf16[8,8,32,1024]{3,1,2,0:T(8,128)(2,1)S(1)} %bitcast.93) | data formatting | bytes 8388608
  25.6 7.6 %all-to-all-start.1 = ((bf16[32,2,32,1024]{3,2,1,0:T(8,128)(2,1)}), bf16[32,2,32,1024]{3,2,1,0:T(8,128)(2,1)}, u32[]{:S(2)}, u32[]{:S(2)}) async-start(bf16[32,2,32,1024]{3,2,1,0:T(8,128)(2,1)} %bitcast.91), calls=%async_computation.1 | async-start | bytes 8388608 | tf_op jit(solution)/shard_map/all_to_all | solution.py:78
  33.4 0.5 broadcast.237
  33.9 0.7 reduce.5
  35.7 49.7 %all-to-all-done.1 = bf16[32,2,32,1024]{3,2,1,0:T(8,128)(2,1)} async-done(((bf16[32,2,32,1024]{3,2,1,0:T(8,128)(2,1)}), bf16[32,2,32,1024]{3,2,1,0:T(8,128)(2,1)}, u32[]{:S(2)}, u32[]{:S(2)}) %all-to-all-start.1) | async-done | bytes 4194336 | tf_op jit(solution)/shard_map/all_to_all | solution.py:78
  85.3 6.8 %copy.51 = bf16[8,8,32,1024]{3,1,2,0:T(8,128)(2,1)} copy(bf16[8,8,32,1024]{3,2,1,0:T(8,128)(2,1)} %bitcast.54) | data formatting | bytes 8388608
  92.1 3.0 convolution_convert_fusion.1
  95.4 4.7 %convolution_add_fusion = bf16[128,4096]{1,0:T(8,128)(2,1)S(1)} fusion(bf16[128,1024]{1,0:T(8,128)(2,1)S(1)} %reshape_reshape.4, bf16[1024,4096]{1,0:T(8,128)(2,1)} %param.15, f32[4096]{0:T(1024)S(1)} %copy-done.3), kind=kOutput, calls=%fused_computation.3 | convolution fusion | flops 1074790400 | bytes 9715712 | tf_op jit(solution)/shard_map/dot_general | solution.py:182
  100.1 0.6 fusion
  100.8 0.3 fusion.2
  101.2 4.3 stack.2
  105.4 8.3 %all-to-all-start.2 = ((bf16[8,4,32,4096]{3,2,1,0:T(8,128)(2,1)}), bf16[8,4,32,4096]{3,2,1,0:T(8,128)(2,1)}, u32[]{:S(2)}, u32[]{:S(2)}) async-start(bf16[8,4,32,4096]{3,2,1,0:T(8,128)(2,1)} %stack.2), calls=%async_computation.2 | async-start | bytes 16777216 | tf_op jit(solution)/shard_map/all_to_all | solution.py:111
  113.9 0.7 pad_maximum_fusion
  115.0 0.3 fusion.22
  115.6 61.8 %all-gather.2.cloned.1.call-done = bf16[4096,768]{0,1:T(8,128)(2,1)} async-done(((bf16[128,768]{0,1:T(8,128)(2,1)}), bf16[4096,768]{0,1:T(8,128)(2,1)}) %all-gather.2.cloned.1.call-update) | async-done | bytes 6291472 | tf_op jit(solution)/shard_map/all_gather | solution.py:33
  177.3 4.7 %slice.36 = bf16[4096,512]{0,1:T(8,128)(2,1)} slice(bf16[4096,768]{0,1:T(8,128)(2,1)} %all-gather.2.cloned.1.call-done), slice={[0:4096], [0:512]} | slice | bytes 8388608 | tf_op jit(solution)/shard_map/slice | solution.py:35
  182.0 118.8 %all-to-all-done.2 = bf16[8,4,32,4096]{3,2,1,0:T(8,128)(2,1)} async-done(((bf16[8,4,32,4096]{3,2,1,0:T(8,128)(2,1)}), bf16[8,4,32,4096]{3,2,1,0:T(8,128)(2,1)}, u32[]{:S(2)}, u32[]{:S(2)}) %all-to-all-start.2) | async-done | bytes 8388640 | tf_op jit(solution)/shard_map/all_to_all | solution.py:111
  300.8 7.7 %copy.35 = bf16[4,8,32,4096]{3,2,1,0:T(8,128)(2,1)} copy(bf16[4,8,32,4096]{3,2,0,1:T(8,128)(2,1)} %bitcast.3) | data formatting | bytes 16777216 | tf_op jit(solution)/shard_map/reshape | solution.py:110
  308.5 8.2 %convolution_bitcast_fusion = f32[4,256,1,4,128]{1,4,3,0,2:T(8,128)S(1)} fusion(bf16[4,256,4096,1]{2,1,3,0:T(8,128)(2,1)} %bitcast.94, bf16[4,128,4096,1]{2,1,0,3:T(8,128)(2,1)} %bitcast.95), kind=kOutput, calls=%fused_computation.17 | convolution fusion | flops 4294967296 | bytes 14680064 | tf_op jit(solution)/shard_map/dot_general | solution.py:115
  317.0 0.5 fusion.4
  317.5 0.6 fusion.5
  318.1 0.8 convolution_convert_fusion.3
  318.9 7.2 %convolution_convert_fusion.2 = bf16[4,256,4096]{2,1,0:T(8,128)(2,1)} fusion(bf16[4,256,256]{1,2,0:T(8,128)(2,1)S(1)} %bitcast.97, bf16[4096,768]{0,1:T(8,128)(2,1)} %all-gather.2.cloned.1.call-done), kind=kOutput, calls=%fused_computation.2 | convolution fusion | flops 2151677952 | bytes 11010048 | tf_op jit(solution)/shard_map/dot_general | solution.py:145
  326.1 90.2 %reduce-scatter.2.cloned.1.call-done = bf16[4,32,4096]{2,1,0:T(8,128)(2,1)} async-done(((bf16[4,256,4096]{2,1,0:T(8,128)(2,1)}), bf16[4,32,4096]{2,1,0:T(8,128)(2,1)}) %reduce-scatter.2.cloned.1.call-update) | async-done | bytes 1048592 | tf_op jit(solution)/shard_map/reduce_scatter | solution.py:151
  416.3 2.4 fusion.3
  (43 shorter events, 2.5 us)
Async XLA Ops:
  7.8 17.8 %all-to-all-start = ((s32[32,1,4]{2,1,0:T(1,128)}), s32[32,1,4]{2,1,0:T(1,128)S(1)}, u32[]{:S(2)}, u32[]{:S(2)}) async-start(s32[32,1,4]{2,1,0:T(1,128)} %broadcast_in_dim.37), calls=%async_computation | async-start | bytes 32768 | tf_op jit(solution)/shard_map/all_to_all | solution.py:16
  25.6 7.6 %copy-start.5 = (s32[4]{0:T(128)S(1)}, s32[4]{0:T(128)}, u32[]{:S(2)}) copy-start(s32[4]{0:T(128)} %param.11) | copy-start | bytes 52
  25.6 7.6 %copy-start.6 = (s32[4]{0:T(128)S(1)}, s32[4]{0:T(128)}, u32[]{:S(2)}) copy-start(s32[4]{0:T(128)} %param.12) | copy-start | bytes 52
  25.6 59.7 %all-to-all-start.1 = ((bf16[32,2,32,1024]{3,2,1,0:T(8,128)(2,1)}), bf16[32,2,32,1024]{3,2,1,0:T(8,128)(2,1)}, u32[]{:S(2)}, u32[]{:S(2)}) async-start(bf16[32,2,32,1024]{3,2,1,0:T(8,128)(2,1)} %bitcast.91), calls=%async_computation.1 | async-start | bytes 8388608 | tf_op jit(solution)/shard_map/all_to_all | solution.py:78
  92.1 3.3 copy-start.3
  95.3 4.8 %copy-start = (bf16[4,32,4096]{2,1,0:T(8,128)(2,1)S(1)}, bf16[4,32,4096]{2,1,0:T(8,128)(2,1)}, u32[]{:S(2)}) copy-start(bf16[4,32,4096]{2,1,0:T(8,128)(2,1)} %param.14) | copy-start | bytes 3145732
  100.1 0.7 copy-start.4
  105.4 8.4 %copy-start.1 = (bf16[1,128,1,512]{3,1,2,0:T(8,128)(2,1)S(1)}, bf16[1,128,1,512]{3,1,2,0:T(8,128)(2,1)}, u32[]{:S(2)}) copy-start(bf16[1,128,1,512]{3,1,2,0:T(8,128)(2,1)} %param.18) | copy-start | bytes 393220
  105.4 8.5 %copy-start.2 = (bf16[1,1,256,128]{3,2,1,0:T(8,128)(2,1)S(1)}, bf16[1,1,256,128]{3,2,1,0:T(8,128)(2,1)}, u32[]{:S(2)}) copy-start(bf16[1,1,256,128]{3,2,1,0:T(8,128)(2,1)} %param.19) | copy-start | bytes 196612
  105.4 195.4 %all-to-all-start.2 = ((bf16[8,4,32,4096]{3,2,1,0:T(8,128)(2,1)}), bf16[8,4,32,4096]{3,2,1,0:T(8,128)(2,1)}, u32[]{:S(2)}, u32[]{:S(2)}) async-start(bf16[8,4,32,4096]{3,2,1,0:T(8,128)(2,1)} %stack.2), calls=%async_computation.2 | async-start | bytes 16777216 | tf_op jit(solution)/shard_map/all_to_all | solution.py:111
  113.7 63.6 %all-gather.2.cloned.1.call-start = ((), (), s32[]{:S(2)}) async-start(), calls=%async_computation.4 | async-start | bytes 6488064 | tf_op jit(solution)/shard_map/all_gather | solution.py:33
  114.6 301.6 %reduce-scatter.2.cloned.1.call-start = ((), (), s32[]{:S(2)}) async-start(), calls=%async_computation.5 | async-start | bytes 9437184 | tf_op jit(solution)/shard_map/reduce_scatter | solution.py:151
Sparse Core Ops, SparseCore 0:
  117.0 60.2 all-gather.1
  326.2 89.9 reduce-scatter.1
